TPU v7x, 512 devices: a whole 4x8x8 slice. The times are simulated.
512 devices in a mesh: rep: 32 (over x_lo, z, core), shard: 16 (over y, x_hi).
Axes of the slice: x: 4 (x_hi: 2, x_lo: 2; x = x_hi * 2 + x_lo), y: 8, z: 8, core: 2. Of those that a mesh axis runs over, the one named last changes fastest.
Arguments:
- outer_delta: float32 [32, 4194304], P('rep', 'shard'), may hold values from -40 to 40
- offsets: int32 [65], replicated, may hold values from 0 to 4194304, as said below
- parameters: float32 [4194304], P('shard'), may hold values from -6 to 6
- momentum: float32 [4194304], P(('shard', 'rep')), may hold values from -1.2 to 1.2
Outputs:
- new_parameters: float32 [4194304], P('shard')
- new_momentum: float32 [4194304], P(('shard', 'rep'))
Inputs may be any that keep to these rules, and one draw needn't show every extreme that they name: `offsets`: strictly increasing multiples of 128, the first 0 and the last 4194304.
All inputs are finite; a program needn't handle non-finite values.
Results may differ from a plain program's by a relative error of at most 0.0003.
Values sent between devices are 32-bit elements; how exact they have to be, the bound alone decides.
A program may use at most 64 MiB of HBM per device.

v0:
```python
import functools
import math

import jax
import jax.numpy as jnp
from jax import lax
from jax.sharding import Mesh
from jax.sharding import PartitionSpec as P

REP = ("rep_0", "rep_1", "rep_2")
SHARD = ("shard_0", "shard_1")
SHARD_REP = ("shard_0", "shard_1", "rep_0", "rep_1", "rep_2")


LR_OUTER = 0.7
MU_OUTER = 0.9
CLIP_RMS = 0.1
EPSILON = 1e-06


def in_blocks(shard, dim, peers):
    lengths = shard.shape
    tiles = shard.reshape(*lengths[:dim], peers, lengths[dim] // peers, *lengths[dim + 1 :])
    return jnp.moveaxis(tiles, dim, 0)


def sent_and_summed(shard, axis, dim):
    tiles = in_blocks(shard, dim, lax.axis_size(axis))
    arrived = lax.all_to_all(tiles, axis, split_axis=0, concat_axis=0, tiled=True)
    return arrived.sum(axis=0)


def one_axis_at_a_time(shard, axes):
    return functools.reduce(lax.psum, axes, shard)


def copy_for_each(shard, axis):
    copies = jnp.broadcast_to(shard, (lax.axis_size(axis), *shard.shape))
    return lax.all_to_all(copies, axis, split_axis=0, concat_axis=0, tiled=True)


def laid_out(tiles, dim):
    lengths = list(tiles.shape[1:])
    lengths[dim] *= tiles.shape[0]
    return jnp.moveaxis(tiles, 0, dim).reshape(lengths)


def gather_directly(shard, axis, dim):
    tiles = copy_for_each(shard, axis)
    return laid_out(tiles, dim)


def one_hot_rows(first_pos, block_len, offsets):
    tensors = offsets.shape[0] - 1
    positions = first_pos + jnp.arange(block_len, dtype=jnp.int32)
    segment = jnp.sum((positions[:, None] >= offsets[None, 1:tensors]).astype(jnp.int32), axis=1)
    return (segment[:, None] == jnp.arange(tensors, dtype=jnp.int32)[None, :]).astype(jnp.float32)


def tensor_squares(values, first_pos, offsets):
    total_len = values.shape[0]
    block_len = math.gcd(total_len, 8192)
    value_rows = values.reshape(total_len // block_len, block_len)
    block_starts = first_pos + jnp.arange(total_len // block_len, dtype=jnp.int32) * block_len

    def partial_squares(items):
        row_values, row_start = items
        selector = one_hot_rows(row_start, block_len, offsets)
        return jnp.dot(
            row_values * row_values,
            selector,
            precision=lax.Precision.HIGHEST,
            preferred_element_type=jnp.float32,
        )

    return jnp.sum(lax.map(partial_squares, (value_rows, block_starts)), axis=0)


def element_factor(factor, total_len, first_pos, offsets):
    block_len = math.gcd(total_len, 8192)
    block_starts = first_pos + jnp.arange(total_len // block_len, dtype=jnp.int32) * block_len

    def spread_factor(row_start):
        selector = one_hot_rows(row_start, block_len, offsets)
        return jnp.dot(
            selector, factor, precision=lax.Precision.HIGHEST, preferred_element_type=jnp.float32
        )

    return lax.map(spread_factor, block_starts).reshape(total_len)


def clip_factor(squares_sum, offsets):
    lengths = (offsets[1:] - offsets[:-1]).astype(jnp.float32)
    return jnp.minimum(1.0, CLIP_RMS * jnp.sqrt(lengths) * lax.rsqrt(squares_sum + EPSILON))


def on_device(outer_delta, offsets, parameters, momentum):
    replicas = lax.axis_size(REP)
    shard_len = parameters.shape[0]
    own_len = shard_len // replicas
    rep_index = lax.axis_index(REP)
    shard_start = lax.axis_index(SHARD) * shard_len
    local_delta = outer_delta.reshape(shard_len)
    avg_delta = sent_and_summed(local_delta, REP, 0) / jnp.float32(replicas)
    first_pos = shard_start + rep_index * own_len
    squares_sum = one_axis_at_a_time(tensor_squares(avg_delta, first_pos, offsets), SHARD_REP)
    factor = clip_factor(squares_sum, offsets)
    scaled = avg_delta * element_factor(factor, own_len, first_pos, offsets)
    owned_params = lax.dynamic_slice_in_dim(parameters, rep_index * own_len, own_len)
    new_momentum = MU_OUTER * momentum + scaled
    new_owned = owned_params - LR_OUTER * (scaled + MU_OUTER * new_momentum)
    new_parameters = gather_directly(new_owned, REP, 0)
    return (new_parameters, new_momentum)


def solution(mesh):
    finer = Mesh(
        mesh.devices.reshape(2, 8, 2, 8, 2), ("rep_0", "rep_1", "rep_2", "shard_0", "shard_1")
    )
    return jax.shard_map(
        on_device,
        mesh=finer,
        in_specs=(P(REP, SHARD), P(), P(SHARD), P(SHARD_REP)),
        out_specs=(P(SHARD), P(SHARD_REP)),
        check_vma=False,
    )
```

profile of v0, /device:TPU:1, one launch (start us, length us, event | category | flops | bytes accessed | tf_op | source)
XLA Modules:
  0.0 126.1 jit_solution(16157995095185665481)
XLA Ops:
  0.6 0.0 copy-start.1
  0.6 12.9 %all-to-all-start = ((f32[32,1,8192]{2,1,0:T(1,128)}), f32[32,1,8192]{2,1,0:T(1,128)S(1)}, u32[]{:S(2)}, u32[]{:S(2)}) async-start(f32[32,1,8192]{2,1,0:T(1,128)} %bitcast.11), calls=%async_computation | async-start | bytes 2097152 | tf_op jit(solution)/shard_map/all_to_all | solution.py:29
  13.6 0.0 copy-done.1
  13.6 0.1 slice.12
  13.6 0.3 convert_reduce_fusion
  14.0 0.0 copy-start
  14.0 26.1 %all-to-all-done = f32[32,1,8192]{2,1,0:T(1,128)S(1)} async-done(((f32[32,1,8192]{2,1,0:T(1,128)}), f32[32,1,8192]{2,1,0:T(1,128)S(1)}, u32[]{:S(2)}, u32[]{:S(2)}) %all-to-all-start) | async-done | bytes 1048608 | tf_op jit(solution)/shard_map/all_to_all | solution.py:29
  40.1 0.7 reduce_sum.22
  40.8 1.0 fusion.2
  41.8 13.9 %psum.35 = f32[64]{0:T(128)S(1)} all-reduce(f32[64]{0:T(128)S(1)} %fusion.2), channel_id=1, replica_groups=mesh['rep_0'=2,'rep_1'=8,'rep_2'=2,'shard_0'=8,'shard_1'=2] {'shard_0'}, use_global_device_ids=true, to_apply=%region_2.3 | all-reduce | flops 64 | bytes 512 | tf_op jit(solution)/shard_map/psum | solution.py:34
  55.7 5.3 %psum.36 = f32[64]{0:T(128)S(1)} all-reduce(f32[64]{0:T(128)S(1)} %psum.35), channel_id=1, replica_groups=mesh['rep_0'=2,'rep_1'=8,'rep_2'=2,'shard_0'=8,'shard_1'=2] {'shard_1'}, use_global_device_ids=true, to_apply=%region_3.4 | all-reduce | flops 64 | bytes 512 | tf_op jit(solution)/shard_map/psum | solution.py:34
  61.0 4.0 %psum.37 = f32[64]{0:T(128)S(1)} all-reduce(f32[64]{0:T(128)S(1)} %psum.36), channel_id=1, replica_groups=mesh['rep_0'=2,'rep_1'=8,'rep_2'=2,'shard_0'=8,'shard_1'=2] {'rep_0'}, use_global_device_ids=true, to_apply=%region_4.5 | all-reduce | flops 64 | bytes 512 | tf_op jit(solution)/shard_map/psum | solution.py:34
  64.9 12.8 %psum.38 = f32[64]{0:T(128)S(1)} all-reduce(f32[64]{0:T(128)S(1)} %psum.37), channel_id=1, replica_groups=mesh['rep_0'=2,'rep_1'=8,'rep_2'=2,'shard_0'=8,'shard_1'=2] {'rep_1'}, use_global_device_ids=true, to_apply=%region_5.6 | all-reduce | flops 64 | bytes 512 | tf_op jit(solution)/shard_map/psum | solution.py:34
  77.7 13.8 %psum.39 = f32[64]{0:T(128)S(1)} all-reduce(f32[64]{0:T(128)S(1)} %psum.38), channel_id=1, replica_groups=mesh['rep_0'=2,'rep_1'=8,'rep_2'=2,'shard_0'=8,'shard_1'=2] {'rep_2'}, use_global_device_ids=true, to_apply=%region_6.7 | all-reduce | flops 64 | bytes 512 | tf_op jit(solution)/shard_map/psum | solution.py:34
  91.5 0.8 fusion
  92.2 0.0 copy-done
  92.2 1.4 %multiply_subtract_fusion = (f32[8192]{0:T(1024)S(1)}, f32[8192]{0:T(1024)}) fusion(f32[262144]{0:T(1024)} %param.6, s32[]{:T(128)S(6)} %select_n.3, f32[8192]{0:T(1024)S(1)} %bitcast.13, f32[8192]{0:T(1024)S(1)} %reduce_sum.22, f32[8192]{0:T(1024)S(1)} %copy-done), kind=kLoop, calls=%fused_computation.7 | loop fusion | flops 65536 | bytes 196612 | tf_op jit(solution)/shard_map/sub | solution.py:111
  93.6 0.9 broadcast_in_dim.27
  94.6 30.5 %all_to_all.15 = f32[32,1,8192]{2,1,0:T(1,128)S(1)} all-to-all(f32[32,1,8192]{2,1,0:T(1,128)S(1)} %broadcast_in_dim.27), channel_id=1, replica_groups=mesh['rep_0'=2,'rep_1'=8,'rep_2'=2,'shard_0'=8,'shard_1'=2] {'rep_0','re..., dimensions={0} | all-to-all | bytes 2097152 | tf_op jit(solution)/shard_map/all_to_all | solution.py:39
  125.0 1.0 copy.7
  (2 shorter events, 0.0 us)
Async XLA Ops:
  0.6 12.9 %copy-start.1 = (s32[65]{0:T(128)S(1)}, s32[65]{0:T(128)}, u32[]{:S(2)}) copy-start(s32[65]{0:T(128)} %param.5) | copy-start | bytes 784
  0.6 39.4 %all-to-all-start = ((f32[32,1,8192]{2,1,0:T(1,128)}), f32[32,1,8192]{2,1,0:T(1,128)S(1)}, u32[]{:S(2)}, u32[]{:S(2)}) async-start(f32[32,1,8192]{2,1,0:T(1,128)} %bitcast.11), calls=%async_computation | async-start | bytes 2097152 | tf_op jit(solution)/shard_map/all_to_all | solution.py:29
  14.0 78.2 %copy-start = (f32[8192]{0:T(1024)S(1)}, f32[8192]{0:T(1024)}, u32[]{:S(2)}) copy-start(f32[8192]{0:T(1024)} %param.7) | copy-start | bytes 98308
where the time goes:
time: 127 us; the launch traced here: 126 us
  blocking collectives  80.1 us (63%)
  waiting for transfers between devices  26.1 us (21%)
  starting transfers between devices  12.9 us (10%)
  other arithmetic  2.43 us (2%)
  local copies, waits for them, and re-layouts  2.05 us (2%)
  matrix products  1.79 us (1%)
    psum x5, blocking collectives, one_axis_at_a_time(): return functools.reduce(lax.psum, axes, shard)  49.7 us
    all_to_all x1, blocking collectives, copy_for_each(): return lax.all_to_all(copies, axis, split_axis=0, concat_axis=0, tiled=True)  30.5 us
    all_to_all x1, waiting for transfers between devices, sent_and_summed(): lax.all_to_all(tiles, axis, split_axis=0, concat_axis=0, tiled=True)  26.1 us
    all_to_all x1, starting transfers between devices, sent_and_summed(): lax.all_to_all(tiles, axis, split_axis=0, concat_axis=0, tiled=True)  12.9 us
  transfers between devices with their start and end apart: 1, of which 1 were waited for; matrix products, arithmetic and copies ran while one was open for 0% of the time, Pallas kernels for 0%

commit v1 on v0

v1 whole, which is shorter than its diff:
```python
import functools

import jax
import jax.numpy as jnp
from jax import lax
from jax.experimental import pallas as pl
from jax.experimental.pallas import tpu as pltpu
from jax.sharding import Mesh
from jax.sharding import PartitionSpec as P

X, Z, CORE, Y, XH = "rep_0", "rep_1", "rep_2", "shard_0", "shard_1"
AXES = (X, Z, CORE, Y, XH)
REP = (X, Z, CORE)
SHARD = (Y, XH)
SHARD_REP = (Y, XH, X, Z, CORE)

LR_OUTER = 0.7
MU_OUTER = 0.9
CLIP_RMS = 0.1
EPSILON = 1e-06


def remote(src, dst, send, recv, dev):
    return pltpu.make_async_remote_copy(
        src_ref=src,
        dst_ref=dst,
        send_sem=send,
        recv_sem=recv,
        device_id=dev,
        device_id_type=pl.DeviceIdType.MESH,
    )


def far_first(n):
    order = [n // 2] if n % 2 == 0 else []
    for d in range((n - 1) // 2, 0, -1):
        order += [d, n - d]
    return order


def step_kernel(
    sizes,
    delta, mom, par, offs,
    newp, newm,
    dl, sib, xs, xr, zs, zr, ga, gm, pv, ov, sqy, sqx, sqz,
    lsem, rs_core, rs_x, rs_z, ag_z, ag_x, ag_core, m_z, m_x, m_core, qy, qx, qz,
):
    nx, nz, nc, ny, nh = (sizes[a] for a in AXES)
    x, z, c, y, h = (lax.axis_index(a) for a in AXES)
    rows = xs.shape[1]
    x_nb, c_nb = {X: 1 - x}, {CORE: 1 - c}
    zof = lambda d: lax.rem(z + d + nz, nz)
    order = far_first(nz)
    nd = len(order)
    mine = x * nz + z

    barrier = pltpu.get_barrier_semaphore()
    z_peers = [{Z: zof(d)} for d in order]
    y_peers = [{Y: lax.rem(y + d, ny)} for d in range(1, ny)]
    x_peers = [
        {XH: lax.rem(h + a, nh), X: lax.rem(x + b, nx), CORE: lax.rem(c + e, nc)}
        for a in range(nh) for b in range(nx) for e in range(nc) if a or b or e
    ]
    peers = z_peers + y_peers + x_peers
    for dev in peers:
        pl.semaphore_signal(barrier, inc=1, device_id=dev, device_id_type=pl.DeviceIdType.MESH)

    load_m = pltpu.make_async_copy(mom, gm.at[mine, c], lsem.at[0])
    load_m.start()
    load_away = pltpu.make_async_copy(delta.at[:, pl.ds(1 - c, 1)], dl.at[:, pl.ds(1 - c, 1)], lsem.at[1])
    load_away.start()
    load_own = pltpu.make_async_copy(delta.at[:, pl.ds(c, 1)], dl.at[:, pl.ds(c, 1)], lsem.at[2])
    load_own.start()
    load_o = pltpu.make_async_copy(offs, ov, lsem.at[3])
    load_o.start()
    load_p = pltpu.make_async_copy(par, pv, lsem.at[4])
    load_p.start()

    load_m.wait()
    load_away.wait()
    pl.semaphore_wait(barrier, len(peers))

    pending = []

    def send(src, dst, sems, i, dev):
        copy = remote(src, dst, sems.at[0, i], sems.at[1, i], dev)
        copy.start()
        pending.append(copy)

    def wait_in(dst, sems, i, dev):
        remote(dst, dst, sems.at[0, i], sems.at[1, i], dev).wait_recv()

    steps = order + [0]
    q_of = lambda xx, i: xx * nz + zof(steps[i])

    for i in range(nz):
        q = q_of(1 - x, i)
        send(dl.at[q, 1 - c], sib.at[q], rs_core, i, c_nb)
    for i in range(nz):
        q = q_of(x, i)
        send(dl.at[q, 1 - c], sib.at[q], rs_core, nz + i, c_nb)

    s = 1 - 2 * c
    na, nb = nz // 2, nz - 1 - nz // 2
    fwd, bwd = {Z: zof(s)}, {Z: zof(-s)}
    origin_a = lambda k: x * nz + zof(-s * k)
    origin_b = lambda k: x * nz + zof(s * k)
    send(gm.at[mine, c], gm.at[mine, c], m_z, 0, fwd)
    send(gm.at[mine, c], gm.at[mine, c], m_z, na, bwd)
    send(gm.at[mine, c], gm.at[mine, c], m_x, 0, x_nb)
    send(gm.at[mine, c], gm.at[mine, c], m_core, 0, c_nb)

    def momentum_step(k):
        if k <= na:
            blk = gm.at[origin_a(k), c]
            wait_in(blk, m_z, k - 1, fwd)
            if k < na:
                send(blk, blk, m_z, k, fwd)
            send(blk, blk, m_x, k, x_nb)
            send(blk, blk, m_core, k, c_nb)
        if k <= nb:
            blk = gm.at[origin_b(k), c]
            wait_in(blk, m_z, na + k - 1, bwd)
            if k < nb:
                send(blk, blk, m_z, na + k, bwd)
            send(blk, blk, m_x, na + k, x_nb)
            send(blk, blk, m_core, na + k, c_nb)

    load_own.wait()

    for i in range(nz):
        q = q_of(1 - x, i)
        wait_in(sib.at[q], rs_core, i, c_nb)
        xs[i] = dl[q, c] + sib[q]
        send(xs.at[i], xr.at[i], rs_x, i, x_nb)

    momentum_step(1)

    for i in range(nz):
        q = q_of(x, i)
        wait_in(sib.at[q], rs_core, nz + i, c_nb)
        part = dl[q, c] + sib[q]
        wait_in(xr.at[i], rs_x, i, x_nb)
        zs[i] = part + xr[i]
        if i < nd:
            send(zs.at[i], zr.at[i], rs_z, i, {Z: zof(steps[i])})
        if i == nz // 2 - 1:
            momentum_step(2)
        if i == nz - 2:
            momentum_step(3)

    total = zs[nz - 1]
    for i in range(nd):
        wait_in(zr.at[i], rs_z, i, z_peers[i])
        total = total + zr[i]
    avg = total * (1.0 / (nx * nz * nc))
    ga[mine, c] = avg

    load_o.wait()
    low = ov[:, 0 : ov.shape[1] - 1]
    high = ov[:, 1 : ov.shape[1]]
    own_len = rows * 128
    shard_pos = (y * nh + h) * (nx * nz * nc * own_len)

    def row_mask(first_pos):
        pos = first_pos + 128 * lax.broadcasted_iota(jnp.int32, (rows, low.shape[1]), 0)
        return (pos >= low) & (pos < high)

    squares = jnp.sum(avg * avg, axis=1, keepdims=True)
    mask = row_mask(shard_pos + (mine * nc + c) * own_len)
    sqy[y] = jnp.sum(jnp.where(mask, squares, 0.0), axis=0, keepdims=True)
    for i, dev in enumerate(y_peers):
        send(sqy.at[y], sqy.at[y], qy, i, dev)

    for i in range(nd):
        send(ga.at[mine, c], ga.at[mine, c], ag_z, i, z_peers[i])
    send(ga.at[mine, c], ga.at[mine, c], ag_x, nd, x_nb)
    send(ga.at[mine, c], ga.at[mine, c], ag_core, nd, c_nb)

    def mean_from_z(i):
        blk = ga.at[x * nz + zof(-steps[i]), c]
        wait_in(blk, ag_z, i, z_peers[i])
        send(blk, blk, ag_x, i, x_nb)
        send(blk, blk, ag_core, i, c_nb)

    def mean_from_x(i):
        blk = ga.at[(1 - x) * nz + zof(-steps[i]), c]
        wait_in(blk, ag_x, i, x_nb)
        send(blk, blk, ag_core, nz + i, c_nb)

    def m_slot(xx, j):
        return xx * nz + (zof(-s * j) if j <= na else zof(s * (j - na)))

    momentum_step(4) if na >= 4 else None
    for j in range(nz):
        blk = gm.at[m_slot(1 - x, j), c]
        wait_in(blk, m_x, j, x_nb)
        send(blk, blk, m_core, nz + j, c_nb)

    for i in range(ny - 1):
        src = lax.rem(y + ny - 1 - i, ny)
        wait_in(sqy.at[src], qy, i, y_peers[i])
    acc = sqy[0]
    for i in range(1, ny):
        acc = acc + sqy[i]
    slot = (h * nx + x) * nc + c
    sqx[slot] = acc
    for i, dev in enumerate(x_peers):
        send(sqx.at[slot], sqx.at[slot], qx, i, dev)

    for i in range(nd):
        mean_from_z(i)

    i = 0
    for a in range(nh):
        for b in range(nx):
            for e in range(nc):
                if a or b or e:
                    hh, xx, cc = lax.rem(h + nh - a, nh), lax.rem(x + nx - b, nx), lax.rem(c + nc - e, nc)
                    wait_in(sqx.at[(hh * nx + xx) * nc + cc], qx, i, x_peers[i])
                    i += 1
    acc = sqx[0]
    for i in range(1, nh * nx * nc):
        acc = acc + sqx[i]
    sqz[z] = acc
    for i in range(nd):
        send(sqz.at[z], sqz.at[z], qz, i, z_peers[i])

    mean_from_x(nd)
    for i in range(nd):
        mean_from_x(i)

    for i in range(nd):
        wait_in(sqz.at[zof(-steps[i])], qz, i, z_peers[i])
    acc = sqz[0]
    for i in range(1, nz):
        acc = acc + sqz[i]
    lengths = (high - low).astype(jnp.float32)
    factor = jnp.minimum(1.0, CLIP_RMS * jnp.sqrt(lengths) * lax.rsqrt(acc + EPSILON))

    for i in range(nz):
        for g, xx in ((0, x), (1, 1 - x)):
            wait_in(ga.at[xx * nz + zof(-steps[i]), 1 - c], ag_core, g * nz + i, c_nb)
    other = -s
    for j in range(nz):
        for g, xx in ((0, x), (1, 1 - x)):
            zz = zof(-other * j) if j <= na else zof(other * (j - na))
            wait_in(gm.at[xx * nz + zz, 1 - c], m_core, g * nz + j, c_nb)

    load_p.wait()
    for copy in pending:
        copy.wait_send()

    def apply(b, carry):
        q, cc = b // nc, lax.rem(b, nc)
        m = row_mask(shard_pos + b * own_len)
        row_factor = jnp.sum(jnp.where(m, factor, 0.0), axis=1, keepdims=True)
        scaled = ga[q, cc] * row_factor
        momentum = MU_OUTER * gm[q, cc] + scaled
        newp[q, cc] = pv[q, cc] - LR_OUTER * (scaled + MU_OUTER * momentum)
        return carry

    lax.fori_loop(0, nx * nz * nc, apply, 0)
    m = row_mask(shard_pos + (mine * nc + c) * own_len)
    row_factor = jnp.sum(jnp.where(m, factor, 0.0), axis=1, keepdims=True)
    newm[...] = MU_OUTER * gm[mine, c] + ga[mine, c] * row_factor


def on_device(sizes, outer_delta, offsets, parameters, momentum):
    nx, nz, nc, ny, nh = (sizes[a] for a in AXES)
    rows = momentum.shape[0] // 128
    nq = nx * nz
    whole = (nq, nc, rows, 128)
    block = (rows, 128)
    f32 = jnp.float32
    dma = lambda n: pltpu.SemaphoreType.DMA((2, n))
    vmem = pltpu.VMEM
    tensors = offsets.shape[0] - 1
    new_parameters, new_momentum = pl.pallas_call(
        functools.partial(step_kernel, sizes),
        out_shape=(jax.ShapeDtypeStruct(whole, f32), jax.ShapeDtypeStruct(block, f32)),
        in_specs=[pl.BlockSpec(memory_space=pl.ANY)] * 4,
        out_specs=(pl.BlockSpec(memory_space=pltpu.VMEM),) * 2,
        scratch_shapes=[
            vmem(whole, f32),
            vmem((nq,) + block, f32),
            vmem((nz,) + block, f32),
            vmem((nz,) + block, f32),
            vmem((nz,) + block, f32),
            vmem((nz,) + block, f32),
            vmem(whole, f32),
            vmem(whole, f32),
            vmem(whole, f32),
            vmem((1, tensors + 1), jnp.int32),
            vmem((ny, 1, tensors), f32),
            vmem((nh * nx * nc, 1, tensors), f32),
            vmem((nz, 1, tensors), f32),
            pltpu.SemaphoreType.DMA((5,)),
            dma(nq), dma(nz), dma(nz), dma(nz), dma(nz), dma(nq), dma(nz), dma(nz), dma(nq),
            dma(ny), dma(nh * nx * nc), dma(nz),
        ],
        compiler_params=pltpu.CompilerParams(
            collective_id=0, has_side_effects=True, vmem_limit_bytes=24 * 1024 * 1024
        ),
    )(
        outer_delta.reshape(whole),
        momentum.reshape(block),
        parameters.reshape(whole),
        offsets.reshape(1, tensors + 1),
    )
    return new_parameters.reshape(parameters.shape), new_momentum.reshape(momentum.shape)


def solution(mesh):
    finer = Mesh(mesh.devices.reshape(2, 8, 2, 8, 2), AXES)
    sizes = dict(finer.shape)
    return jax.shard_map(
        functools.partial(on_device, sizes),
        mesh=finer,
        in_specs=(P(REP, SHARD), P(), P(SHARD), P(SHARD_REP)),
        out_specs=(P(SHARD), P(SHARD_REP)),
        check_vma=False,
    )
```

time: 127 us -> 55.9 us (0.44)
  blocking collectives: 80.1 us -> 0 us
  Pallas kernels: 0 us -> 49.5 us
  waiting for transfers between devices: 26.1 us -> 0 us
  starting transfers between devices: 12.9 us -> 0 us
  local copies, waits for them, and re-layouts: 2.05 us -> 5.51 us
  other arithmetic: 2.43 us -> 0 us
  matrix products: 1.79 us -> 0 us
    psum x5 -> x0, blocking collectives: 49.7 us -> none  [one_axis_at_a_time(): return functools.reduce(lax.psum, axes, shard)]
    pallas_call x0 -> x1, Pallas kernels: none -> 49.5 us  [on_device(): pl.pallas_call(functools.partial(step_kernel, sizes), out_shape=(jax.Shap...]
    all_to_all x1 -> x0, blocking collectives: 30.5 us -> none  [copy_for_each(): return lax.all_to_all(copies, axis, split_axis=0, concat_axis=0, tiled=True)]
    all_to_all x1 -> x0, waiting for transfers between devices: 26.1 us -> none  [sent_and_summed(): lax.all_to_all(tiles, axis, split_axis=0, concat_axis=0, tiled=True)]
    all_to_all x1 -> x0, starting transfers between devices: 12.9 us -> none  [sent_and_summed(): lax.all_to_all(tiles, axis, split_axis=0, concat_axis=0, tiled=True)]
    unnamed x5 -> x10, local copies, waits for them, and re-layouts: 1.05 us -> 5.51 us
    dot_general x2 -> x0, matrix products: 1.79 us -> none  [the longest x1 1.04 us: partial_squares(): jnp.dot(row_values * row_values, selector, precision=lax.Precision.HIGHES...]
    sub x1 -> x0, other arithmetic: 1.39 us -> none  [on_device(): new_owned = owned_params - LR_OUTER * (scaled + MU_OUTER * new_momentum)]
  transfers between devices with their start and end apart: 1 -> 0, of which waited for: 1 -> 0; matrix products, arithmetic and copies ran while one was open for 0% -> 0% of each run, Pallas kernels for 0% -> 0%
where the time goes in v1:
time: 55.9 us; the launch traced here: 55.6 us
  Pallas kernels  49.5 us (89%)
  local copies, waits for them, and re-layouts  5.51 us (10%)
  between operations  0.65 us (1%)
    pallas_call x1, Pallas kernels, on_device(): pl.pallas_call(functools.partial(step_kernel, sizes), out_shape=(jax.Shap...  49.5 us
    unnamed x10, local copies, waits for them, and re-layouts  5.51 us

profile of v1, /device:TPU:1, one launch (start us, length us, event | category | flops | bytes accessed | tf_op | source)
XLA Modules:
  0.0 55.6 jit_solution(8053761973134735831)
XLA Ops:
  0.6 0.0 copy-start.3
  0.6 0.6 %copy-done.3 = s32[65]{0:T(128)S(1)} copy-done((s32[65]{0:T(128)S(1)}, s32[65]{0:T(128)}, u32[]{:S(2)}) %copy-start.3) | copy-done | bytes 284
  1.3 0.0 copy-start
  1.3 1.2 %copy-done = f32[1,262144]{1,0:T(1,128)S(1)} copy-done((f32[1,262144]{1,0:T(1,128)S(1)}, f32[1,262144]{1,0:T(1,128)}, u32[]{:S(2)}) %copy-start) | copy-done | bytes 1048600
  2.5 0.0 copy-start.1
  2.5 1.2 %copy-done.1 = f32[262144]{0:T(1024)S(1)} copy-done((f32[262144]{0:T(1024)S(1)}, f32[262144]{0:T(1024)}, u32[]{:S(2)}) %copy-start.1) | copy-done | bytes 1048600
  3.7 0.0 copy-start.2
  3.7 0.8 %copy-done.2 = f32[8192]{0:T(1024)S(1)} copy-done((f32[8192]{0:T(1024)S(1)}, f32[8192]{0:T(1024)}, u32[]{:S(2)}) %copy-start.2) | copy-done | bytes 32792
  4.5 49.5 %shard_map.59 = (f32[16,2,64,128]{3,2,1,0:T(8,128)S(1)}, f32[64,128]{1,0:T(8,128)S(1)}) custom-call(f32[16,2,64,128]{3,2,1,0:T(8,128)S(1)} %bitcast.6, f32[64,128]{1,0:T(8,128)S(1)} %bitcast.9, f32[16,2,64,128]{3,2,1,0:T(8,128)S(1)} %bitcast.7, s32[1,65]{1,0:T(1,128)S(1)} %bitcast.11), custom_call_target="tpu_custom_call" | custom-call | tf_op jit(solution)/shard_map/pallas_call | solution.py:279
  54.0 1.0 %copy.8 = f32[262144]{0:T(1024)} copy(f32[262144]{0:T(1024)S(1)} %bitcast.8) | data formatting | bytes 2097152
  55.0 0.6 %copy.9 = f32[8192]{0:T(1024)} copy(f32[8192]{0:T(1024)S(1)} %bitcast.10) | data formatting | bytes 65536
Async XLA Ops:
  0.6 0.7 %copy-start.3 = (s32[65]{0:T(128)S(1)}, s32[65]{0:T(128)}, u32[]{:S(2)}) copy-start(s32[65]{0:T(128)} %param.5) | copy-start | bytes 784
  1.3 1.2 %copy-start = (f32[1,262144]{1,0:T(1,128)S(1)}, f32[1,262144]{1,0:T(1,128)}, u32[]{:S(2)}) copy-start(f32[1,262144]{1,0:T(1,128)} %param.4) | copy-start | bytes 3145732
  2.5 1.2 %copy-start.1 = (f32[262144]{0:T(1024)S(1)}, f32[262144]{0:T(1024)}, u32[]{:S(2)}) copy-start(f32[262144]{0:T(1024)} %param.6) | copy-start | bytes 3145732
  3.7 0.8 %copy-start.2 = (f32[8192]{0:T(1024)S(1)}, f32[8192]{0:T(1024)}, u32[]{:S(2)}) copy-start(f32[8192]{0:T(1024)} %param.7) | copy-start | bytes 98308

commit v2 on v0

v2 whole, which is shorter than its diff:
```python
import functools

import jax
import jax.numpy as jnp
from jax import lax
from jax.experimental import pallas as pl
from jax.experimental.pallas import tpu as pltpu
from jax.sharding import Mesh
from jax.sharding import PartitionSpec as P

X, Z, CORE, Y, XH = "rep_0", "rep_1", "rep_2", "shard_0", "shard_1"
AXES = (X, Z, CORE, Y, XH)
REP = (X, Z, CORE)
SHARD = (Y, XH)
SHARD_REP = (Y, XH, X, Z, CORE)

LR_OUTER = 0.7
MU_OUTER = 0.9
CLIP_RMS = 0.1
EPSILON = 1e-06


def remote(src, dst, send, recv, dev):
    return pltpu.make_async_remote_copy(
        src_ref=src,
        dst_ref=dst,
        send_sem=send,
        recv_sem=recv,
        device_id=dev,
        device_id_type=pl.DeviceIdType.MESH,
    )


def rs_order(half):
    order = [half]
    for d in range(half - 1, 0, -1):
        order += [-d, d]
    if half > 2:
        order.remove(half - 1)
        order.insert(half, half - 1)
    return order + [0]


def ag_order(half):
    return [e * d for d in range(1, half) for e in (1, -1)]


def step_kernel(
    sizes,
    delta, mom, par, offs,
    newp, newm,
    dl, sib, xs, xr, zs, zr, ar, ga, gm, pv, ov, hot, fac, sq1, sq2,
    lsem, c_send, c_far, c_near, x_send, x_recv, z_send, z_recv, a_send, a_recv,
    gz_send, gz_recv, gx_send, gx_recv, gc_send, gc_col, gc_recv,
    mx_send, mx_recv, mz_send, mz_recv, mc_send, mc_recv, q_send, q_recv,
):
    nx, nz, nc, ny, nh = (sizes[a] for a in AXES)
    x, z, c, y, h = (lax.axis_index(a) for a in AXES)
    rows = xs.shape[1]
    nq, half = nx * nz, nz // 2
    scope = jax.named_scope
    s = 1 - 2 * c
    zof = lambda d: lax.rem(z + s * d + nz, nz)
    mine, near, away = x * nz + z, x * nz, (1 - x) * nz
    x_nb, c_nb = {X: 1 - x}, {CORE: 1 - c}
    z_dev = lambda d: {Z: zof(d)}

    barrier = pltpu.get_barrier_semaphore()
    peers1 = [
        {Y: lax.rem(y + a, ny), CORE: lax.rem(c + b, nc)}
        for a in range(ny) for b in range(nc) if a or b
    ]
    peers2 = [
        {XH: lax.rem(h + a, nh), X: lax.rem(x + b, nx), Z: lax.rem(z + e, nz)}
        for a in range(nh) for b in range(nx) for e in range(nz) if a or b or e
    ]
    load_m = pltpu.make_async_copy(mom, gm.at[mine, c], lsem.at[0])
    load_m.start()
    load_away = pltpu.make_async_copy(delta.at[:, pl.ds(1 - c, 1)], dl.at[:, pl.ds(1 - c, 1)], lsem.at[1])
    load_away.start()
    load_own = pltpu.make_async_copy(delta.at[:, pl.ds(c, 1)], dl.at[:, pl.ds(c, 1)], lsem.at[2])
    load_own.start()
    with scope("signal"):
        for dev in peers1 + peers2:
            pl.semaphore_signal(barrier, inc=1, device_id=dev, device_id_type=pl.DeviceIdType.MESH)
    load_o = pltpu.make_async_copy(offs, ov, lsem.at[3])
    load_o.start()
    load_p = pltpu.make_async_copy(par, pv, lsem.at[4])
    load_p.start()
    with scope("load"):
        load_m.wait()
        load_away.wait()
    with scope("barrier"):
        pl.semaphore_wait(barrier, len(peers1) + len(peers2))

    def send(src, dst, send_sem, recv_sem, dev):
        remote(src, dst, send_sem, recv_sem, dev).start()

    def sent(ref, send_sem):
        remote(ref, ref, send_sem, send_sem, c_nb).wait_send()

    def came(ref, recv_sem):
        remote(ref, ref, recv_sem, recv_sem, c_nb).wait_recv()

    def all_of(ref, count):
        return ref.at[pl.ds(0, count)]

    send(gm.at[mine, c], gm.at[mine, c], mx_send, mx_recv, x_nb)

    def momentum_send(d, to, i):
        for first in (near, away):
            blk = gm.at[first + zof(d), c]
            send(blk, blk, mz_send, mz_recv.at[i], z_dev(to))

    def momentum_step(k):
        if k > 1:
            came(all_of(xs, 2), mz_recv.at[k - 2])
            if k <= half:
                came(all_of(xs, 2), mz_recv.at[half + k - 2])
        if k <= half:
            momentum_send(1 - k, 1, k - 1)
        if k < half:
            momentum_send(k - 1, -1, half + k - 1)

    steps = rs_order(half)
    with scope("core_send"):
        for i in range(nz):
            q = away + zof(-steps[i])
            send(dl.at[q, 1 - c], sib.at[q], c_send, c_far.at[i], c_nb)
        column = pl.ds(near, nz)
        send(dl.at[column, 1 - c], sib.at[column], c_send, c_near, c_nb)
        load_own.wait()

    with scope("x_stage"):
        for i in range(nz):
            q = away + zof(steps[i])
            came(sib.at[q], c_far.at[i])
            xs[i] = dl[q, c] + sib[q]
            send(xs.at[i], xr.at[i], x_send, x_recv.at[i], x_nb)

    own_len = rows * 128
    shard_pos = (y * nh + h) * (nq * nc * own_len)
    tensors = ov.shape[1] - 1
    with scope("one_hot"):
        load_o.wait()
        low, high = ov[:, 0:tensors], ov[:, 1 : tensors + 1]
        low, high = jnp.concatenate([low, low], axis=1), jnp.concatenate([high, high], axis=1)
        lanes = 2 * tensors

        def row_mask(first_pos):
            pos = first_pos + 128 * lax.broadcasted_iota(jnp.int32, (rows, lanes), 0)
            return (pos >= low) & (pos < high)

        for b in range(nq * nc):
            inside = row_mask(shard_pos + b * own_len)
            hot[pl.ds(b * rows, rows), :] = jnp.where(inside, 1.0, 0.0).astype(jnp.bfloat16)

    with scope("m1"):
        came(gm.at[away + z, c], mx_recv)
        momentum_step(1)

    came(sib.at[column], c_near)
    for i in range(nz):
        d = steps[i]
        with scope(f"z_stage{i}"):
            q = near + zof(d)
            came(xr.at[i], x_recv.at[i])
            part = dl[q, c] + sib[q] + xr[i]
            if d == half - 1:
                came(ar, a_recv)
                part = part + ar[...]
            zs[i] = part
            if i == 0:
                send(zs.at[i], ar, a_send, a_recv, z_dev(1))
            elif d != 0:
                send(zs.at[i], zr.at[i - 1], z_send, z_recv, z_dev(d))
        if i == half:
            with scope("m2"):
                momentum_step(2)
    with scope("m3"):
        if half > 2:
            momentum_step(3)

    with scope("z_sum"):
        came(zr, z_recv)
        total = zs[nz - 1]
        for i in range(nz - 2):
            total = total + zr[i]
        avg = total * (1.0 / (nq * nc))
        ga[mine, c] = avg

    slot1 = y * nc + c
    with scope("squares"):
        squares = jnp.sum(avg * avg, axis=1, keepdims=True)
        mask = row_mask(shard_pos + (mine * nc + c) * own_len)
        sq1[slot1] = jnp.sum(jnp.where(mask, squares, 0.0), axis=0, keepdims=True)
        for dev in peers1:
            send(sq1.at[slot1], sq1.at[slot1], q_send.at[0], q_recv.at[0], dev)

    hops = ag_order(half)
    nh_ = len(hops)
    own = ga.at[mine, c]
    with scope("ag_send"):
        for i, d in enumerate(hops):
            send(own, own, gz_send, gz_recv.at[i], z_dev(d))
        send(own, own, gx_send, gx_recv.at[nh_ + 1], x_nb)

    def mean_from_z(i):
        d = hops[i] if i < nh_ else half
        blk = ga.at[near + zof(-d), c]
        came(blk, gz_recv.at[i])
        if d == half - 1:
            send(blk, blk, gz_send, gz_recv.at[nh_], z_dev(1))
        send(blk, blk, gx_send, gx_recv.at[i], x_nb)

    def mean_from_x(i):
        d = 0 if i > nh_ else half if i == nh_ else hops[i]
        blk = ga.at[away + zof(-d), c]
        came(blk, gx_recv.at[i])
        send(blk, blk, gc_send, gc_recv.at[i], c_nb)

    for i in range(min(2, nh_)):
        with scope(f"ag_z{i}"):
            mean_from_z(i)

    slot2 = (h * nx + x) * nz + z
    with scope("q1"):
        came(all_of(sq1, ny * nc - 1), q_recv.at[0])
        acc = sq1[0]
        for i in range(1, ny * nc):
            acc = acc + sq1[i]
        sq2[slot2] = acc
        for dev in peers2:
            send(sq2.at[slot2], sq2.at[slot2], q_send.at[1], q_recv.at[1], dev)

    for i in range(2, nh_):
        with scope(f"ag_z{i}"):
            mean_from_z(i)
    with scope("ag_x_own"):
        mean_from_x(nh_ + 1)
    with scope("m4"):
        for k in range(4, half + 1):
            momentum_step(k)
    with scope("ag_z_far"):
        mean_from_z(nh_)
        send(ga.at[column, c], ga.at[column, c], gc_send, gc_col, c_nb)
    for i in range(2):
        with scope(f"ag_x{i}"):
            mean_from_x(i)
    with scope("m5"):
        momentum_step(half + 1)
        send(gm.at[:, c], gm.at[:, c], mc_send, mc_recv, c_nb)
    for i in range(2, nh_ + 1):
        with scope(f"ag_x{i}"):
            mean_from_x(i)

    with scope("q2"):
        came(all_of(sq2, nh * nq - 1), q_recv.at[1])
        acc = sq2[0]
        for i in range(1, nh * nq):
            acc = acc + sq2[i]
    with scope("factor"):
        lengths = (high - low).astype(jnp.float32)
        factor = jnp.minimum(1.0, CLIP_RMS * jnp.sqrt(lengths) * lax.rsqrt(acc + EPSILON))
        at = lambda axis: lax.broadcasted_iota(jnp.int32, (tensors, lanes), axis)
        spread = jnp.sum(jnp.where(at(0) == at(1), factor, 0.0), axis=1, keepdims=True)
        spread = jnp.broadcast_to(spread, (tensors, 128))
        upper = spread.astype(jnp.bfloat16)
        fac[0:tensors, :] = upper
        fac[tensors:lanes, :] = (spread - upper.astype(jnp.float32)).astype(jnp.bfloat16)
        table = fac[...]

    with scope("m_core"):
        came(gm.at[:, 1 - c], mc_recv)
    with scope("base"):
        load_p.wait()
        for q in range(nq):
            pv[q] = pv[q] - (LR_OUTER * MU_OUTER * MU_OUTER) * gm[q]

    with scope("ag_core"):
        came(ga.at[column, 1 - c], gc_col)
        for i in range(nz):
            d = 0 if i > nh_ else half if i == nh_ else hops[i]
            came(ga.at[away + zof(d), 1 - c], gc_recv.at[i])

    with scope("apply"):
        step = 2
        for b in range(0, nq, step):
            spread = jnp.dot(
                hot[pl.ds(b * nc * rows, step * nc * rows), :], table, preferred_element_type=jnp.float32
            ).reshape(step, nc, rows, 128)
            part = pl.ds(b, step)
            newp[part] = pv[part] - (LR_OUTER * (1.0 + MU_OUTER)) * (ga[part] * spread)
        first = pl.multiple_of((mine * nc + c) * rows, rows)
        spread = jnp.dot(hot[pl.ds(first, rows), :], table, preferred_element_type=jnp.float32)
        newm[...] = MU_OUTER * gm[mine, c] + ga[mine, c] * spread

    with scope("drain"):
        sent(sib, c_send)
        sent(xs, x_send)
        sent(zr, z_send)
        sent(ar, a_send)
        sent(all_of(xs, nz - 1), gz_send)
        sent(xs, gx_send)
        sent(sib, gc_send)
        sent(ar, mx_send)
        sent(all_of(sib, 2 * (nz - 1)), mz_send)
        sent(sib, mc_send)
        sent(all_of(sq1, ny * nc - 1), q_send.at[0])
        sent(all_of(sq2, nh * nq - 1), q_send.at[1])


def write_out(newp, newm, out_p, out_m, sem):
    copies = [pltpu.make_async_copy(newp, out_p, sem.at[0]), pltpu.make_async_copy(newm, out_m, sem.at[1])]
    for copy in copies:
        copy.start()
    for copy in copies:
        copy.wait()


VMEM_LIMIT = 52 * 1024 * 1024


def on_device(sizes, outer_delta, offsets, parameters, momentum):
    nx, nz, nc, ny, nh = (sizes[a] for a in AXES)
    rows = momentum.shape[0] // 128
    nq = nx * nz
    whole = (nq, nc, rows, 128)
    block = (rows, 128)
    f32 = jnp.float32
    dma = lambda *n: pltpu.SemaphoreType.DMA(n)
    vmem = pltpu.VMEM
    tensors = offsets.shape[0] - 1
    outs = (jax.ShapeDtypeStruct(whole, f32), jax.ShapeDtypeStruct(block, f32))
    in_vmem = (pl.BlockSpec(memory_space=pltpu.VMEM),) * 2
    results = pl.pallas_call(
        functools.partial(step_kernel, sizes),
        out_shape=outs,
        in_specs=[pl.BlockSpec(memory_space=pltpu.HBM)] * 4,
        out_specs=in_vmem,
        scratch_shapes=[
            vmem(whole, f32),
            vmem((nq,) + block, f32),
            vmem((nz,) + block, f32),
            vmem((nz,) + block, f32),
            vmem((nz,) + block, f32),
            vmem((nz - 2,) + block, f32),
            vmem(block, f32),
            vmem(whole, f32),
            vmem(whole, f32),
            vmem(whole, f32),
            vmem((1, tensors + 1), jnp.int32),
            vmem((nq * nc * rows, 2 * tensors), jnp.bfloat16),
            vmem((2 * tensors, 128), jnp.bfloat16),
            vmem((ny * nc, 1, 2 * tensors), f32),
            vmem((nh * nq, 1, 2 * tensors), f32),
            dma(5),
            dma(), dma(nz), dma(),
            dma(), dma(nz),
            dma(), dma(), dma(), dma(),
            dma(), dma(nz - 1), dma(), dma(nz), dma(), dma(), dma(nz),
            dma(), dma(), dma(), dma(nz - 1), dma(), dma(),
            dma(2), dma(2),
        ],
        compiler_params=pltpu.CompilerParams(
            collective_id=0, has_side_effects=True, vmem_limit_bytes=VMEM_LIMIT
        ),
    )(
        outer_delta.reshape(whole),
        momentum.reshape(block),
        parameters.reshape(whole),
        offsets.reshape(1, tensors + 1),
    )
    new_parameters, new_momentum = pl.pallas_call(
        write_out,
        out_shape=outs,
        in_specs=list(in_vmem),
        out_specs=(pl.BlockSpec(memory_space=pl.ANY),) * 2,
        scratch_shapes=[dma(2)],
        compiler_params=pltpu.CompilerParams(vmem_limit_bytes=4 * 1024 * 1024),
    )(*results)
    return new_parameters.reshape(parameters.shape), new_momentum.reshape(momentum.shape)


def solution(mesh):
    finer = Mesh(mesh.devices.reshape(2, 8, 2, 8, 2), AXES)
    sizes = dict(finer.shape)
    return jax.shard_map(
        functools.partial(on_device, sizes),
        mesh=finer,
        in_specs=(P(REP, SHARD), P(), P(SHARD), P(SHARD_REP)),
        out_specs=(P(SHARD), P(SHARD_REP)),
        check_vma=False,
    )
```

time: 127 us -> 46.4 us (0.37)
  blocking collectives: 80.1 us -> 0 us
  Pallas kernels: 0 us -> 44.2 us
  waiting for transfers between devices: 26.1 us -> 0 us
  starting transfers between devices: 12.9 us -> 0 us
  other arithmetic: 2.43 us -> 0 us
  matrix products: 1.79 us -> 0 us
    psum x5 -> x0, blocking collectives: 49.7 us -> none  [one_axis_at_a_time(): return functools.reduce(lax.psum, axes, shard)]
    pallas_call x0 -> x2, Pallas kernels: none -> 44.2 us  [the longest x1 43.2 us: on_device(): pl.pallas_call(functools.partial(step_kernel, sizes), out_shape=outs, in_...]
    all_to_all x1 -> x0, blocking collectives: 30.5 us -> none  [copy_for_each(): return lax.all_to_all(copies, axis, split_axis=0, concat_axis=0, tiled=True)]
    all_to_all x1 -> x0, waiting for transfers between devices: 26.1 us -> none  [sent_and_summed(): lax.all_to_all(tiles, axis, split_axis=0, concat_axis=0, tiled=True)]
    all_to_all x1 -> x0, starting transfers between devices: 12.9 us -> none  [sent_and_summed(): lax.all_to_all(tiles, axis, split_axis=0, concat_axis=0, tiled=True)]
    dot_general x2 -> x0, matrix products: 1.79 us -> none  [the longest x1 1.04 us: partial_squares(): jnp.dot(row_values * row_values, selector, precision=lax.Precision.HIGHES...]
    sub x1 -> x0, other arithmetic: 1.39 us -> none  [on_device(): new_owned = owned_params - LR_OUTER * (scaled + MU_OUTER * new_momentum)]
  transfers between devices with their start and end apart: 1 -> 0, of which waited for: 1 -> 0; matrix products, arithmetic and copies ran while one was open for 0% -> 0% of each run, Pallas kernels for 0% -> 0%
where the time goes in v2:
time: 46.4 us; the launch traced here: 46.2 us
  Pallas kernels  44.2 us (95%)
  local copies, waits for them, and re-layouts  1.41 us (3%)
  between operations  0.65 us (1%)
    pallas_call x1, Pallas kernels, on_device(): pl.pallas_call(functools.partial(step_kernel, sizes), out_shape=outs, in_...  43.2 us
    unnamed x4, local copies, waits for them, and re-layouts  1.41 us
    pallas_call x1, Pallas kernels, on_device(): pl.pallas_call(write_out, out_shape=outs, in_specs=list(in_vmem), out_spe...  0.99 us

profile of v2, /device:TPU:1, one launch (start us, length us, event | category | flops | bytes accessed | tf_op | source)
XLA Modules:
  0.0 46.2 jit_solution(17294523650263200452)
XLA Ops:
  0.6 0.0 copy-start.1
  0.6 0.6 %copy-done.1 = s32[65]{0:T(128)S(1)} copy-done((s32[65]{0:T(128)S(1)}, s32[65]{0:T(128)}, u32[]{:S(2)}) %copy-start.1) | copy-done | bytes 284
  1.3 0.0 copy-start
  1.3 0.8 %copy-done = f32[8192]{0:T(1024)S(1)} copy-done((f32[8192]{0:T(1024)S(1)}, f32[8192]{0:T(1024)}, u32[]{:S(2)}) %copy-start) | copy-done | bytes 32792
  2.0 43.2 %shard_map.59 = (f32[16,2,64,128]{3,2,1,0:T(8,128)S(1)}, f32[64,128]{1,0:T(8,128)S(1)}) custom-call(f32[16,2,64,128]{3,2,1,0:T(8,128)} %bitcast.8, f32[64,128]{1,0:T(8,128)S(1)} %bitcast.6, f32[16,2,64,128]{3,2,1,0:T(8,128)} %bitcast.9, s32[1,65]{1,0:T(1,128)S(1)} %bitcast.7), custom_call_target="tpu_custom_call" | custom-call | tf_op jit(solution)/shard_map/pallas_call | solution.py:336
  45.2 1.0 %shard_map.60 = (f32[16,2,64,128]{3,2,1,0:T(8,128)}, f32[64,128]{1,0:T(8,128)}) custom-call(f32[16,2,64,128]{3,2,1,0:T(8,128)S(1)} %get-tuple-element.6.newp, f32[64,128]{1,0:T(8,128)S(1)} %get-tuple-element.7.newm), custom_call_target="tpu_custom_call" | custom-call | tf_op jit(solution)/shard_map/pallas_call | solution.py:374
Async XLA Ops:
  0.6 0.7 %copy-start.1 = (s32[65]{0:T(128)S(1)}, s32[65]{0:T(128)}, u32[]{:S(2)}) copy-start(s32[65]{0:T(128)} %param.5) | copy-start | bytes 784
  1.3 0.8 %copy-start = (f32[8192]{0:T(1024)S(1)}, f32[8192]{0:T(1024)}, u32[]{:S(2)}) copy-start(f32[8192]{0:T(1024)} %param.7) | copy-start | bytes 98308

commit v3 on v2

--- a/solution.py
+++ b/solution.py
@@ -41,10 +41,6 @@
     return order + [0]
 
 
-def ag_order(half):
-    return [e * d for d in range(1, half) for e in (1, -1)]
-
-
 def step_kernel(
     sizes,
     delta, mom, par, offs,
@@ -52,7 +48,7 @@
     dl, sib, xs, xr, zs, zr, ar, ga, gm, pv, ov, hot, fac, sq1, sq2,
     lsem, c_send, c_far, c_near, x_send, x_recv, z_send, z_recv, a_send, a_recv,
     gz_send, gz_recv, gx_send, gx_recv, gc_send, gc_col, gc_recv,
-    mx_send, mx_recv, mz_send, mz_recv, mc_send, mc_recv, q_send, q_recv,
+    mx_send, mx_recv, mz_send, mz_recv, mc_send, mc_recv, q_send, q_recv, in_column, in_peers,
 ):
     nx, nz, nc, ny, nh = (sizes[a] for a in AXES)
     x, z, c, y, h = (lax.axis_index(a) for a in AXES)
@@ -62,6 +58,7 @@
     s = 1 - 2 * c
     zof = lambda d: lax.rem(z + s * d + nz, nz)
     mine, near, away = x * nz + z, x * nz, (1 - x) * nz
+    column = pl.ds(near, nz)
     x_nb, c_nb = {X: 1 - x}, {CORE: 1 - c}
     z_dev = lambda d: {Z: zof(d)}
 
@@ -74,6 +71,28 @@
         {XH: lax.rem(h + a, nh), X: lax.rem(x + b, nx), Z: lax.rem(z + e, nz)}
         for a in range(nh) for b in range(nx) for e in range(nz) if a or b or e
     ]
+    row = [
+        {XH: lax.rem(h + a, nh), X: lax.rem(x + b, nx)}
+        for a in range(nh) for b in range(nx) if a or b
+    ]
+    cores = [{CORE: e} for e in range(nc)]
+
+    def tell(sem, dev):
+        pl.semaphore_signal(sem, inc=1, device_id=dev, device_id_type=pl.DeviceIdType.MESH)
+
+    def tell_each(sem, axis, first, last, devs):
+        def at(i, carry):
+            for dev in devs:
+                tell(sem, dev | {axis: i})
+            return carry
+
+        lax.fori_loop(first, last, at, 0)
+
+    def wait_for(sem, count):
+        @pl.when(count > 0)
+        def _():
+            pl.semaphore_wait(sem, count)
+
     load_m = pltpu.make_async_copy(mom, gm.at[mine, c], lsem.at[0])
     load_m.start()
     load_away = pltpu.make_async_copy(delta.at[:, pl.ds(1 - c, 1)], dl.at[:, pl.ds(1 - c, 1)], lsem.at[1])
@@ -81,8 +100,10 @@
     load_own = pltpu.make_async_copy(delta.at[:, pl.ds(c, 1)], dl.at[:, pl.ds(c, 1)], lsem.at[2])
     load_own.start()
     with scope("signal"):
-        for dev in peers1 + peers2:
-            pl.semaphore_signal(barrier, inc=1, device_id=dev, device_id_type=pl.DeviceIdType.MESH)
+        for dev in [c_nb] + row:
+            tell(barrier, dev)
+        tell_each(barrier, Z, z + 1, nz, [{}] + row)
+        tell_each(barrier, Y, y + 1, ny, cores)
     load_o = pltpu.make_async_copy(offs, ov, lsem.at[3])
     load_o.start()
     load_p = pltpu.make_async_copy(par, pv, lsem.at[4])
@@ -91,7 +112,8 @@
         load_m.wait()
         load_away.wait()
     with scope("barrier"):
-        pl.semaphore_wait(barrier, len(peers1) + len(peers2))
+        pl.semaphore_wait(barrier, 1 + len(row) + y * nc + z * (1 + len(row)))
+        tell_each(in_column, Z, 0, z, [{}])
 
     def send(src, dst, send_sem, recv_sem, dev):
         remote(src, dst, send_sem, recv_sem, dev).start()
@@ -105,32 +127,40 @@
     def all_of(ref, count):
         return ref.at[pl.ds(0, count)]
 
-    send(gm.at[mine, c], gm.at[mine, c], mx_send, mx_recv, x_nb)
-
-    def momentum_send(d, to, i):
-        for first in (near, away):
-            blk = gm.at[first + zof(d), c]
-            send(blk, blk, mz_send, mz_recv.at[i], z_dev(to))
-
-    def momentum_step(k):
-        if k > 1:
-            came(all_of(xs, 2), mz_recv.at[k - 2])
-            if k <= half:
-                came(all_of(xs, 2), mz_recv.at[half + k - 2])
-        if k <= half:
-            momentum_send(1 - k, 1, k - 1)
-        if k < half:
-            momentum_send(k - 1, -1, half + k - 1)
+    own_m = gm.at[mine, c]
+    near_m = [e * d for d in range(1, max(half - 1, 2)) for e in (1, -1)]
+    last = near_m[-2]
+    passed = [(-last, 1), (-last, 2), (last, -1)] if half > 2 else [(-last, 1)]
+    send(own_m, own_m, mx_send, mx_recv, x_nb)
+    def momentum_across(d):
+        blk = gm.at[near + zof(d), c]
+        send(blk, blk, mx_send, mx_recv, x_nb)
+
+    def momentum_near():
+        came(all_of(xs, len(near_m)), mz_recv.at[0])
+        for d, to in passed:
+            blk = gm.at[near + zof(d), c]
+            send(blk, blk, mz_send, mz_recv.at[1], z_dev(to))
+        for d in near_m:
+            momentum_across(-d)
+
+    def momentum_far():
+        came(all_of(xs, len(passed)), mz_recv.at[1])
+        for d, to in passed:
+            momentum_across(d - to)
+        send(gm.at[column, c], gm.at[column, c], mc_send, mc_recv, c_nb)
 
     steps = rs_order(half)
     with scope("core_send"):
         for i in range(nz):
             q = away + zof(-steps[i])
             send(dl.at[q, 1 - c], sib.at[q], c_send, c_far.at[i], c_nb)
-        column = pl.ds(near, nz)
         send(dl.at[column, 1 - c], sib.at[column], c_send, c_near, c_nb)
         load_own.wait()
 
+    with scope("tell"):
+        tell_each(in_peers, Z, 0, z, row)
+        tell_each(in_peers, Y, 0, y, cores)
     with scope("x_stage"):
         for i in range(nz):
             q = away + zof(steps[i])
@@ -155,10 +185,10 @@
             inside = row_mask(shard_pos + b * own_len)
             hot[pl.ds(b * rows, rows), :] = jnp.where(inside, 1.0, 0.0).astype(jnp.bfloat16)
 
-    with scope("m1"):
-        came(gm.at[away + z, c], mx_recv)
-        momentum_step(1)
-
+    with scope("column"):
+        wait_for(in_column, nz - 1 - z)
+        for d in near_m:
+            send(own_m, own_m, mz_send, mz_recv.at[0], z_dev(d))
     came(sib.at[column], c_near)
     for i in range(nz):
         d = steps[i]
@@ -174,12 +204,8 @@
                 send(zs.at[i], ar, a_send, a_recv, z_dev(1))
             elif d != 0:
                 send(zs.at[i], zr.at[i - 1], z_send, z_recv, z_dev(d))
-        if i == half:
-            with scope("m2"):
-                momentum_step(2)
-    with scope("m3"):
-        if half > 2:
-            momentum_step(3)
+    with scope("m_near"):
+        momentum_near()
 
     with scope("z_sum"):
         came(zr, z_recv)
@@ -194,32 +220,34 @@
         squares = jnp.sum(avg * avg, axis=1, keepdims=True)
         mask = row_mask(shard_pos + (mine * nc + c) * own_len)
         sq1[slot1] = jnp.sum(jnp.where(mask, squares, 0.0), axis=0, keepdims=True)
+        wait_for(in_peers, (ny - 1 - y) * nc + (nz - 1 - z) * len(row))
         for dev in peers1:
             send(sq1.at[slot1], sq1.at[slot1], q_send.at[0], q_recv.at[0], dev)
 
-    hops = ag_order(half)
-    nh_ = len(hops)
     own = ga.at[mine, c]
+    from_z = [-d for d in near_m] + [d - to for d, to in passed]
+    origins = from_z + [0]
     with scope("ag_send"):
-        for i, d in enumerate(hops):
+        for i, d in enumerate(near_m):
             send(own, own, gz_send, gz_recv.at[i], z_dev(d))
-        send(own, own, gx_send, gx_recv.at[nh_ + 1], x_nb)
+        send(own, own, gx_send, gx_recv.at[nz - 1], x_nb)
 
     def mean_from_z(i):
-        d = hops[i] if i < nh_ else half
-        blk = ga.at[near + zof(-d), c]
+        blk = ga.at[near + zof(from_z[i]), c]
         came(blk, gz_recv.at[i])
-        if d == half - 1:
-            send(blk, blk, gz_send, gz_recv.at[nh_], z_dev(1))
+        for k, (d, to) in enumerate(passed):
+            if d == from_z[i]:
+                send(blk, blk, gz_send, gz_recv.at[len(near_m) + k], z_dev(to))
         send(blk, blk, gx_send, gx_recv.at[i], x_nb)
 
     def mean_from_x(i):
-        d = 0 if i > nh_ else half if i == nh_ else hops[i]
-        blk = ga.at[away + zof(-d), c]
+        blk = ga.at[away + zof(origins[i]), c]
         came(blk, gx_recv.at[i])
         send(blk, blk, gc_send, gc_recv.at[i], c_nb)
 
-    for i in range(min(2, nh_)):
+    with scope("m_far"):
+        momentum_far()
+    for i in range(len(near_m)):
         with scope(f"ag_z{i}"):
             mean_from_z(i)
 
@@ -233,24 +261,20 @@
         for dev in peers2:
             send(sq2.at[slot2], sq2.at[slot2], q_send.at[1], q_recv.at[1], dev)
 
-    for i in range(2, nh_):
-        with scope(f"ag_z{i}"):
-            mean_from_z(i)
     with scope("ag_x_own"):
-        mean_from_x(nh_ + 1)
-    with scope("m4"):
-        for k in range(4, half + 1):
-            momentum_step(k)
-    with scope("ag_z_far"):
-        mean_from_z(nh_)
-        send(ga.at[column, c], ga.at[column, c], gc_send, gc_col, c_nb)
+        mean_from_x(nz - 1)
     for i in range(2):
         with scope(f"ag_x{i}"):
             mean_from_x(i)
-    with scope("m5"):
-        momentum_step(half + 1)
-        send(gm.at[:, c], gm.at[:, c], mc_send, mc_recv, c_nb)
-    for i in range(2, nh_ + 1):
+    for i in range(len(near_m), nz - 1):
+        with scope(f"ag_z{i}"):
+            mean_from_z(i)
+    send(ga.at[column, c], ga.at[column, c], gc_send, gc_col, c_nb)
+    with scope("m_x"):
+        other = gm.at[pl.ds(away, nz), c]
+        came(other, mx_recv)
+        send(other, other, mc_send, mc_recv, c_nb)
+    for i in range(2, nz - 1):
         with scope(f"ag_x{i}"):
             mean_from_x(i)
 
@@ -280,8 +304,7 @@
     with scope("ag_core"):
         came(ga.at[column, 1 - c], gc_col)
         for i in range(nz):
-            d = 0 if i > nh_ else half if i == nh_ else hops[i]
-            came(ga.at[away + zof(d), 1 - c], gc_recv.at[i])
+            came(ga.at[away + zof(-origins[i]), 1 - c], gc_recv.at[i])
 
     with scope("apply"):
         step = 2
@@ -303,8 +326,8 @@
         sent(all_of(xs, nz - 1), gz_send)
         sent(xs, gx_send)
         sent(sib, gc_send)
-        sent(ar, mx_send)
-        sent(all_of(sib, 2 * (nz - 1)), mz_send)
+        sent(xs, mx_send)
+        sent(all_of(xs, nz - 1), mz_send)
         sent(sib, mc_send)
         sent(all_of(sq1, ny * nc - 1), q_send.at[0])
         sent(all_of(sq2, nh * nq - 1), q_send.at[1])
@@ -359,8 +382,8 @@
             dma(), dma(nz),
             dma(), dma(), dma(), dma(),
             dma(), dma(nz - 1), dma(), dma(nz), dma(), dma(), dma(nz),
-            dma(), dma(), dma(), dma(nz - 1), dma(), dma(),
-            dma(2), dma(2),
+            dma(), dma(), dma(), dma(2), dma(), dma(),
+            dma(2), dma(2), pltpu.SemaphoreType.REGULAR, pltpu.SemaphoreType.REGULAR,
         ],
         compiler_params=pltpu.CompilerParams(
             collective_id=0, has_side_effects=True, vmem_limit_bytes=VMEM_LIMIT

time: 46.4 us -> 43.2 us (0.931)
  Pallas kernels: 44.2 us -> 40.6 us
    pallas_call x1, Pallas kernels: 43.2 us -> 39.6 us  [on_device(): pl.pallas_call(functools.partial(step_kernel, sizes), out_shape=outs, in_...]
where the time goes in v3:
time: 43.2 us; the launch traced here: 42.6 us
  Pallas kernels  40.6 us (94%)
  local copies, waits for them, and re-layouts  1.41 us (3%)
  between operations  0.65 us (2%)
    pallas_call x1, Pallas kernels, on_device(): pl.pallas_call(functools.partial(step_kernel, sizes), out_shape=outs, in_...  39.6 us
    unnamed x4, local copies, waits for them, and re-layouts  1.41 us
    pallas_call x1, Pallas kernels, on_device(): pl.pallas_call(write_out, out_shape=outs, in_specs=list(in_vmem), out_spe...  0.99 us

profile of v3, /device:TPU:1, one launch (start us, length us, event | category | flops | bytes accessed | tf_op | source)
XLA Modules:
  0.0 42.6 jit_solution(4658467579789573493)
XLA Ops:
  0.6 0.0 copy-start.1
  0.6 0.6 %copy-done.1 = s32[65]{0:T(128)S(1)} copy-done((s32[65]{0:T(128)S(1)}, s32[65]{0:T(128)}, u32[]{:S(2)}) %copy-start.1) | copy-done | bytes 284
  1.3 0.0 copy-start
  1.3 0.8 %copy-done = f32[8192]{0:T(1024)S(1)} copy-done((f32[8192]{0:T(1024)S(1)}, f32[8192]{0:T(1024)}, u32[]{:S(2)}) %copy-start) | copy-done | bytes 32792
  2.0 39.6 %shard_map.59 = (f32[16,2,64,128]{3,2,1,0:T(8,128)S(1)}, f32[64,128]{1,0:T(8,128)S(1)}) custom-call(f32[16,2,64,128]{3,2,1,0:T(8,128)} %bitcast.8, f32[64,128]{1,0:T(8,128)S(1)} %bitcast.6, f32[16,2,64,128]{3,2,1,0:T(8,128)} %bitcast.9, s32[1,65]{1,0:T(1,128)S(1)} %bitcast.7), custom_call_target="tpu_custom_call" | custom-call | tf_op jit(solution)/shard_map/pallas_call | solution.py:359
  41.6 1.0 %shard_map.60 = (f32[16,2,64,128]{3,2,1,0:T(8,128)}, f32[64,128]{1,0:T(8,128)}) custom-call(f32[16,2,64,128]{3,2,1,0:T(8,128)S(1)} %get-tuple-element.6.newp, f32[64,128]{1,0:T(8,128)S(1)} %get-tuple-element.7.newm), custom_call_target="tpu_custom_call" | custom-call | tf_op jit(solution)/shard_map/pallas_call | solution.py:397
Async XLA Ops:
  0.6 0.7 %copy-start.1 = (s32[65]{0:T(128)S(1)}, s32[65]{0:T(128)}, u32[]{:S(2)}) copy-start(s32[65]{0:T(128)} %param.5) | copy-start | bytes 784
  1.3 0.8 %copy-start = (f32[8192]{0:T(1024)S(1)}, f32[8192]{0:T(1024)}, u32[]{:S(2)}) copy-start(f32[8192]{0:T(1024)} %param.7) | copy-start | bytes 98308

commit v4 on v3

--- a/solution.py
+++ b/solution.py
@@ -75,6 +75,7 @@
         {XH: lax.rem(h + a, nh), X: lax.rem(x + b, nx)}
         for a in range(nh) for b in range(nx) if a or b
     ]
+    pair = [{X: b} for b in range(nx)]
     cores = [{CORE: e} for e in range(nc)]
 
     def tell(sem, dev):
@@ -100,8 +101,9 @@
     load_own = pltpu.make_async_copy(delta.at[:, pl.ds(c, 1)], dl.at[:, pl.ds(c, 1)], lsem.at[2])
     load_own.start()
     with scope("signal"):
-        for dev in [c_nb] + row:
+        for dev in (c_nb, x_nb):
             tell(barrier, dev)
+        tell_each(barrier, XH, h + 1, nh, pair)
         tell_each(barrier, Z, z + 1, nz, [{}] + row)
         tell_each(barrier, Y, y + 1, ny, cores)
     load_o = pltpu.make_async_copy(offs, ov, lsem.at[3])
@@ -112,8 +114,13 @@
         load_m.wait()
         load_away.wait()
     with scope("barrier"):
-        pl.semaphore_wait(barrier, 1 + len(row) + y * nc + z * (1 + len(row)))
-        tell_each(in_column, Z, 0, z, [{}])
+        pl.semaphore_wait(barrier, 2 + h * nx + y * nc + z * (1 + len(row)))
+
+        def tell_column(i, carry):
+            tell(in_column.at[z - 1 - i], {Z: i})
+            return carry
+
+        lax.fori_loop(0, z, tell_column, 0)
 
     def send(src, dst, send_sem, recv_sem, dev):
         remote(src, dst, send_sem, recv_sem, dev).start()
@@ -132,6 +139,13 @@
     last = near_m[-2]
     passed = [(-last, 1), (-last, 2), (last, -1)] if half > 2 else [(-last, 1)]
     send(own_m, own_m, mx_send, mx_recv, x_nb)
+    reach = max(near_m)
+
+    def momentum_to(i, condition):
+        @pl.when(condition)
+        def _():
+            send(own_m, own_m, mz_send, mz_recv.at[0], {Z: i})
+
     def momentum_across(d):
         blk = gm.at[near + zof(d), c]
         send(blk, blk, mx_send, mx_recv, x_nb)
@@ -158,7 +172,11 @@
         send(dl.at[column, 1 - c], sib.at[column], c_send, c_near, c_nb)
         load_own.wait()
 
+    with scope("m_smaller"):
+        for d in near_m:
+            momentum_to(zof(d), zof(d) < z)
     with scope("tell"):
+        tell_each(in_peers, XH, 0, h, pair)
         tell_each(in_peers, Z, 0, z, row)
         tell_each(in_peers, Y, 0, y, cores)
     with scope("x_stage"):
@@ -186,9 +204,15 @@
             hot[pl.ds(b * rows, rows), :] = jnp.where(inside, 1.0, 0.0).astype(jnp.bfloat16)
 
     with scope("column"):
-        wait_for(in_column, nz - 1 - z)
-        for d in near_m:
-            send(own_m, own_m, mz_send, mz_recv.at[0], z_dev(d))
+        for e in range(1, nz):
+            @pl.when(z + e < nz)
+            def _(e=e):
+                pl.semaphore_wait(in_column.at[e - 1], 1)
+
+            if e <= reach:
+                momentum_to(z + e, z + e < nz)
+        for e in range(1, reach + 1):
+            momentum_to(z - e + nz, z - e < 0)
     came(sib.at[column], c_near)
     for i in range(nz):
         d = steps[i]
@@ -220,63 +244,104 @@
         squares = jnp.sum(avg * avg, axis=1, keepdims=True)
         mask = row_mask(shard_pos + (mine * nc + c) * own_len)
         sq1[slot1] = jnp.sum(jnp.where(mask, squares, 0.0), axis=0, keepdims=True)
-        wait_for(in_peers, (ny - 1 - y) * nc + (nz - 1 - z) * len(row))
+        wait_for(in_peers, (nh - 1 - h) * nx + (ny - 1 - y) * nc + (nz - 1 - z) * len(row))
         for dev in peers1:
             send(sq1.at[slot1], sq1.at[slot1], q_send.at[0], q_recv.at[0], dev)
 
     own = ga.at[mine, c]
-    from_z = [-d for d in near_m] + [d - to for d, to in passed]
+    hops = [e * d for d in list(range(2, half)) + [1] for e in (1, -1)]
+    relay = -min(2, half - 1)
+    from_z = [-d for d in hops] + [-half]
     origins = from_z + [0]
+    beyond = [i for i in range(2, nz - 2) if abs(from_z[i]) > 1]
+    beside = [i for i in range(2, nz - 2) if abs(from_z[i]) == 1]
     with scope("ag_send"):
-        for i, d in enumerate(near_m):
+        for i, d in enumerate(hops):
+            if i in beside:
+                continue
             send(own, own, gz_send, gz_recv.at[i], z_dev(d))
         send(own, own, gx_send, gx_recv.at[nz - 1], x_nb)
 
     def mean_from_z(i):
         blk = ga.at[near + zof(from_z[i]), c]
         came(blk, gz_recv.at[i])
-        for k, (d, to) in enumerate(passed):
-            if d == from_z[i]:
-                send(blk, blk, gz_send, gz_recv.at[len(near_m) + k], z_dev(to))
-        send(blk, blk, gx_send, gx_recv.at[i], x_nb)
+        if from_z[i] == relay:
+            send(blk, blk, gz_send, gz_recv.at[nz - 2], z_dev(half + relay))
+        if abs(from_z[i]) > 1:
+            send(blk, blk, gx_send, gx_recv.at[i], x_nb)
+
+    def mean_beside():
+        across = ga.at[away + z, c]
+        for k, d in enumerate(from_z):
+            if abs(d) == 1:
+                if k in beside:
+                    send(own, own, gz_send, gz_recv.at[k], z_dev(-d))
+                send(across, across, gx_send, gx_recv.at[k], z_dev(-d))
 
     def mean_from_x(i):
         blk = ga.at[away + zof(origins[i]), c]
         came(blk, gx_recv.at[i])
-        send(blk, blk, gc_send, gc_recv.at[i], c_nb)
+        if origins[i] == 0 and half == 2:
+            mean_beside()
+        send(blk, blk, gc_send, gc_recv, c_nb)
+
+    slot2 = (h * nx + x) * nz + z
+
+    def exchange_squares(condition):
+        @pl.when(condition)
+        def _():
+            with scope("q1"):
+                came(all_of(sq1, ny * nc - 1), q_recv.at[0])
+                acc = sq1[0]
+                for i in range(1, ny * nc):
+                    acc = acc + sq1[i]
+                sq2[slot2] = acc
+                for dev in peers2:
+                    send(sq2.at[slot2], sq2.at[slot2], q_send.at[1], q_recv.at[1], dev)
+                if half > 2:
+                    mean_beside()
 
     with scope("m_far"):
         momentum_far()
-    for i in range(len(near_m)):
+    with scope("ag_x_own"):
+        mean_from_x(nz - 1)
+    exchange_squares(2 * y >= ny)
+    for i in [0, 1] + beyond:
         with scope(f"ag_z{i}"):
             mean_from_z(i)
 
-    slot2 = (h * nx + x) * nz + z
-    with scope("q1"):
-        came(all_of(sq1, ny * nc - 1), q_recv.at[0])
-        acc = sq1[0]
-        for i in range(1, ny * nc):
-            acc = acc + sq1[i]
-        sq2[slot2] = acc
-        for dev in peers2:
-            send(sq2.at[slot2], sq2.at[slot2], q_send.at[1], q_recv.at[1], dev)
-
-    with scope("ag_x_own"):
-        mean_from_x(nz - 1)
-    for i in range(2):
-        with scope(f"ag_x{i}"):
-            mean_from_x(i)
-    for i in range(len(near_m), nz - 1):
+    exchange_squares(2 * y < ny)
+    for i in [nz - 2] + beside:
         with scope(f"ag_z{i}"):
             mean_from_z(i)
     send(ga.at[column, c], ga.at[column, c], gc_send, gc_col, c_nb)
+    with scope("drain1"):
+        sent(sib, c_send)
+        sent(xs, x_send)
+        sent(zr, z_send)
+        sent(ar, a_send)
+        sent(all_of(xs, nz - 1), gz_send)
+        sent(all_of(xs, nz - 1), mz_send)
+        sent(all_of(sq1, ny * nc - 1), q_send.at[0])
+    for i in [0, 1] + beside:
+        with scope(f"ag_x{i}"):
+            mean_from_x(i)
     with scope("m_x"):
         other = gm.at[pl.ds(away, nz), c]
         came(other, mx_recv)
         send(other, other, mc_send, mc_recv, c_nb)
-    for i in range(2, nz - 1):
+    for i in beyond:
         with scope(f"ag_x{i}"):
             mean_from_x(i)
+
+    with scope("m_core"):
+        came(gm.at[:, 1 - c], mc_recv)
+    with scope("base"):
+        load_p.wait()
+        for q in range(nq):
+            pv[q] = pv[q] - (LR_OUTER * MU_OUTER * MU_OUTER) * gm[q]
+    with scope("ag_x_far"):
+        mean_from_x(nz - 2)
 
     with scope("q2"):
         came(all_of(sq2, nh * nq - 1), q_recv.at[1])
@@ -294,17 +359,9 @@
         fac[tensors:lanes, :] = (spread - upper.astype(jnp.float32)).astype(jnp.bfloat16)
         table = fac[...]
 
-    with scope("m_core"):
-        came(gm.at[:, 1 - c], mc_recv)
-    with scope("base"):
-        load_p.wait()
-        for q in range(nq):
-            pv[q] = pv[q] - (LR_OUTER * MU_OUTER * MU_OUTER) * gm[q]
-
     with scope("ag_core"):
         came(ga.at[column, 1 - c], gc_col)
-        for i in range(nz):
-            came(ga.at[away + zof(-origins[i]), 1 - c], gc_recv.at[i])
+        came(xs, gc_recv)
 
     with scope("apply"):
         step = 2
@@ -314,22 +371,15 @@
             ).reshape(step, nc, rows, 128)
             part = pl.ds(b, step)
             newp[part] = pv[part] - (LR_OUTER * (1.0 + MU_OUTER)) * (ga[part] * spread)
-        first = pl.multiple_of((mine * nc + c) * rows, rows)
-        spread = jnp.dot(hot[pl.ds(first, rows), :], table, preferred_element_type=jnp.float32)
+        row0 = pl.multiple_of((mine * nc + c) * rows, rows)
+        spread = jnp.dot(hot[pl.ds(row0, rows), :], table, preferred_element_type=jnp.float32)
         newm[...] = MU_OUTER * gm[mine, c] + ga[mine, c] * spread
 
     with scope("drain"):
-        sent(sib, c_send)
-        sent(xs, x_send)
-        sent(zr, z_send)
-        sent(ar, a_send)
-        sent(all_of(xs, nz - 1), gz_send)
         sent(xs, gx_send)
         sent(sib, gc_send)
         sent(xs, mx_send)
-        sent(all_of(xs, nz - 1), mz_send)
         sent(sib, mc_send)
-        sent(all_of(sq1, ny * nc - 1), q_send.at[0])
         sent(all_of(sq2, nh * nq - 1), q_send.at[1])
 
 
@@ -381,9 +431,9 @@
             dma(), dma(nz), dma(),
             dma(), dma(nz),
             dma(), dma(), dma(), dma(),
-            dma(), dma(nz - 1), dma(), dma(nz), dma(), dma(), dma(nz),
+            dma(), dma(nz - 1), dma(), dma(nz), dma(), dma(), dma(),
             dma(), dma(), dma(), dma(2), dma(), dma(),
-            dma(2), dma(2), pltpu.SemaphoreType.REGULAR, pltpu.SemaphoreType.REGULAR,
+            dma(2), dma(2), pltpu.SemaphoreType.REGULAR((nz - 1,)), pltpu.SemaphoreType.REGULAR,
         ],
         compiler_params=pltpu.CompilerParams(
             collective_id=0, has_side_effects=True, vmem_limit_bytes=VMEM_LIMIT

time: 43.2 us -> 41.5 us (0.961)
  Pallas kernels: 40.6 us -> 39.3 us
    pallas_call x1, Pallas kernels: 39.6 us -> 38.3 us  [on_device(): pl.pallas_call(functools.partial(step_kernel, sizes), out_shape=outs, in_...]
where the time goes in v4:
time: 41.5 us; the launch traced here: 41.3 us
  Pallas kernels  39.3 us (95%)
  local copies, waits for them, and re-layouts  1.41 us (3%)
  between operations  0.65 us (2%)
    pallas_call x1, Pallas kernels, on_device(): pl.pallas_call(functools.partial(step_kernel, sizes), out_shape=outs, in_...  38.3 us
    unnamed x4, local copies, waits for them, and re-layouts  1.41 us
    pallas_call x1, Pallas kernels, on_device(): pl.pallas_call(write_out, out_shape=outs, in_specs=list(in_vmem), out_spe...  0.99 us

profile of v4, /device:TPU:1, one launch (start us, length us, event | category | flops | bytes accessed | tf_op | source)
XLA Modules:
  0.0 41.3 jit_solution(11372902520780339438)
XLA Ops:
  0.6 0.0 copy-start.1
  0.6 0.6 %copy-done.1 = s32[65]{0:T(128)S(1)} copy-done((s32[65]{0:T(128)S(1)}, s32[65]{0:T(128)}, u32[]{:S(2)}) %copy-start.1) | copy-done | bytes 284
  1.3 0.0 copy-start
  1.3 0.8 %copy-done = f32[8192]{0:T(1024)S(1)} copy-done((f32[8192]{0:T(1024)S(1)}, f32[8192]{0:T(1024)}, u32[]{:S(2)}) %copy-start) | copy-done | bytes 32792
  2.0 38.3 %shard_map.59 = (f32[16,2,64,128]{3,2,1,0:T(8,128)S(1)}, f32[64,128]{1,0:T(8,128)S(1)}) custom-call(f32[16,2,64,128]{3,2,1,0:T(8,128)} %bitcast.8, f32[64,128]{1,0:T(8,128)S(1)} %bitcast.6, f32[16,2,64,128]{3,2,1,0:T(8,128)} %bitcast.9, s32[1,65]{1,0:T(1,128)S(1)} %bitcast.7), custom_call_target="tpu_custom_call" | custom-call | tf_op jit(solution)/shard_map/pallas_call | solution.py:409
  40.3 1.0 %shard_map.60 = (f32[16,2,64,128]{3,2,1,0:T(8,128)}, f32[64,128]{1,0:T(8,128)}) custom-call(f32[16,2,64,128]{3,2,1,0:T(8,128)S(1)} %get-tuple-element.6.newp, f32[64,128]{1,0:T(8,128)S(1)} %get-tuple-element.7.newm), custom_call_target="tpu_custom_call" | custom-call | tf_op jit(solution)/shard_map/pallas_call | solution.py:447
Async XLA Ops:
  0.6 0.7 %copy-start.1 = (s32[65]{0:T(128)S(1)}, s32[65]{0:T(128)}, u32[]{:S(2)}) copy-start(s32[65]{0:T(128)} %param.5) | copy-start | bytes 784
  1.3 0.8 %copy-start = (f32[8192]{0:T(1024)S(1)}, f32[8192]{0:T(1024)}, u32[]{:S(2)}) copy-start(f32[8192]{0:T(1024)} %param.7) | copy-start | bytes 98308

commit v5 on v4

--- a/solution.py
+++ b/solution.py
@@ -214,20 +214,29 @@
         for e in range(1, reach + 1):
             momentum_to(z - e + nz, z - e < 0)
     came(sib.at[column], c_near)
+
+    def carrier(i, condition):
+        @pl.when(condition)
+        def _():
+            came(ar, a_recv)
+            zs[i] = zs[i] + ar[...]
+            send(zs.at[i], zr.at[i - 1], z_send, z_recv, z_dev(half - 1))
+
     for i in range(nz):
         d = steps[i]
         with scope(f"z_stage{i}"):
             q = near + zof(d)
             came(xr.at[i], x_recv.at[i])
             part = dl[q, c] + sib[q] + xr[i]
-            if d == half - 1:
-                came(ar, a_recv)
-                part = part + ar[...]
             zs[i] = part
             if i == 0:
                 send(zs.at[i], ar, a_send, a_recv, z_dev(1))
+            elif d == half - 1:
+                carrier(i, 2 * z >= nz)
             elif d != 0:
                 send(zs.at[i], zr.at[i - 1], z_send, z_recv, z_dev(d))
+    with scope("carrier"):
+        carrier(steps.index(half - 1), 2 * z < nz)
     with scope("m_near"):
         momentum_near()
 
@@ -298,14 +307,14 @@
                 sq2[slot2] = acc
                 for dev in peers2:
                     send(sq2.at[slot2], sq2.at[slot2], q_send.at[1], q_recv.at[1], dev)
-                if half > 2:
-                    mean_beside()
 
     with scope("m_far"):
         momentum_far()
     with scope("ag_x_own"):
         mean_from_x(nz - 1)
     exchange_squares(2 * y >= ny)
+    if half > 2:
+        mean_beside()
     for i in [0, 1] + beyond:
         with scope(f"ag_z{i}"):
             mean_from_z(i)
@@ -315,6 +324,10 @@
         with scope(f"ag_z{i}"):
             mean_from_z(i)
     send(ga.at[column, c], ga.at[column, c], gc_send, gc_col, c_nb)
+    with scope("m_x"):
+        other = gm.at[pl.ds(away, nz), c]
+        came(other, mx_recv)
+        send(other, other, mc_send, mc_recv, c_nb)
     with scope("drain1"):
         sent(sib, c_send)
         sent(xs, x_send)
@@ -326,10 +339,6 @@
     for i in [0, 1] + beside:
         with scope(f"ag_x{i}"):
             mean_from_x(i)
-    with scope("m_x"):
-        other = gm.at[pl.ds(away, nz), c]
-        came(other, mx_recv)
-        send(other, other, mc_send, mc_recv, c_nb)
     for i in beyond:
         with scope(f"ag_x{i}"):
             mean_from_x(i)

time: 41.5 us -> 40.6 us (0.978)
  the two profiles are of different devices: /device:TPU:1 before, /device:TPU:57 now
where the time goes in v5:
time: 40.6 us; the launch traced here: 40.3 us
  Pallas kernels  38.3 us (94%)
  local copies, waits for them, and re-layouts  1.41 us (3%)
  between operations  0.65 us (2%)
    pallas_call x1, Pallas kernels, on_device(): pl.pallas_call(functools.partial(step_kernel, sizes), out_shape=outs, in_...  37.3 us
    unnamed x4, local copies, waits for them, and re-layouts  1.41 us
    pallas_call x1, Pallas kernels, on_device(): pl.pallas_call(write_out, out_shape=outs, in_specs=list(in_vmem), out_spe...  0.99 us

profile of v5, /device:TPU:57, one launch (start us, length us, event | category | flops | bytes accessed | tf_op | source)
XLA Modules:
  0.0 40.3 jit_solution(15586669519805406860)
XLA Ops:
  0.6 0.0 copy-start.1
  0.6 0.6 %copy-done.1 = s32[65]{0:T(128)S(1)} copy-done((s32[65]{0:T(128)S(1)}, s32[65]{0:T(128)}, u32[]{:S(2)}) %copy-start.1) | copy-done | bytes 284
  1.3 0.0 copy-start
  1.3 0.8 %copy-done = f32[8192]{0:T(1024)S(1)} copy-done((f32[8192]{0:T(1024)S(1)}, f32[8192]{0:T(1024)}, u32[]{:S(2)}) %copy-start) | copy-done | bytes 32792
  2.0 37.3 %shard_map.59 = (f32[16,2,64,128]{3,2,1,0:T(8,128)S(1)}, f32[64,128]{1,0:T(8,128)S(1)}) custom-call(f32[16,2,64,128]{3,2,1,0:T(8,128)} %bitcast.8, f32[64,128]{1,0:T(8,128)S(1)} %bitcast.6, f32[16,2,64,128]{3,2,1,0:T(8,128)} %bitcast.9, s32[1,65]{1,0:T(1,128)S(1)} %bitcast.7), custom_call_target="tpu_custom_call" | custom-call | tf_op jit(solution)/shard_map/pallas_call | solution.py:418
  39.4 1.0 %shard_map.60 = (f32[16,2,64,128]{3,2,1,0:T(8,128)}, f32[64,128]{1,0:T(8,128)}) custom-call(f32[16,2,64,128]{3,2,1,0:T(8,128)S(1)} %get-tuple-element.6.newp, f32[64,128]{1,0:T(8,128)S(1)} %get-tuple-element.7.newm), custom_call_target="tpu_custom_call" | custom-call | tf_op jit(solution)/shard_map/pallas_call | solution.py:456
Async XLA Ops:
  0.6 0.7 %copy-start.1 = (s32[65]{0:T(128)S(1)}, s32[65]{0:T(128)}, u32[]{:S(2)}) copy-start(s32[65]{0:T(128)} %param.5) | copy-start | bytes 784
  1.3 0.8 %copy-start = (f32[8192]{0:T(1024)S(1)}, f32[8192]{0:T(1024)}, u32[]{:S(2)}) copy-start(f32[8192]{0:T(1024)} %param.7) | copy-start | bytes 98308

commit v6 on v5

--- a/solution.py
+++ b/solution.py
@@ -278,6 +278,8 @@
             send(blk, blk, gz_send, gz_recv.at[nz - 2], z_dev(half + relay))
         if abs(from_z[i]) > 1:
             send(blk, blk, gx_send, gx_recv.at[i], x_nb)
+        if i == nz - 2:
+            send(blk, blk, gc_send, gc_recv, {X: 1 - x, CORE: 1 - c})
 
     def mean_beside():
         across = ga.at[away + z, c]
@@ -292,7 +294,8 @@
         came(blk, gx_recv.at[i])
         if origins[i] == 0 and half == 2:
             mean_beside()
-        send(blk, blk, gc_send, gc_recv, c_nb)
+        if i != nz - 2:
+            send(blk, blk, gc_send, gc_recv, c_nb)
 
     slot2 = (h * nx + x) * nz + z
 
@@ -313,11 +316,11 @@
     with scope("ag_x_own"):
         mean_from_x(nz - 1)
     exchange_squares(2 * y >= ny)
-    if half > 2:
-        mean_beside()
     for i in [0, 1] + beyond:
         with scope(f"ag_z{i}"):
             mean_from_z(i)
+        if i == 1 and half > 2:
+            mean_beside()
 
     exchange_squares(2 * y < ny)
     for i in [nz - 2] + beside:

time: 40.6 us -> 40 us (0.985)
  the two profiles are of different devices: /device:TPU:57 before, /device:TPU:1 now
where the time goes in v6:
time: 40 us; the launch traced here: 39.8 us
  Pallas kernels  37.7 us (94%)
  local copies, waits for them, and re-layouts  1.41 us (4%)
  between operations  0.65 us (2%)
    pallas_call x1, Pallas kernels, on_device(): pl.pallas_call(functools.partial(step_kernel, sizes), out_shape=outs, in_...  36.8 us
    unnamed x4, local copies, waits for them, and re-layouts  1.41 us
    pallas_call x1, Pallas kernels, on_device(): pl.pallas_call(write_out, out_shape=outs, in_specs=list(in_vmem), out_spe...  0.99 us

profile of v6, /device:TPU:1, one launch (start us, length us, event | category | flops | bytes accessed | tf_op | source)
XLA Modules:
  0.0 39.8 jit_solution(9785866870805587289)
XLA Ops:
  0.6 0.0 copy-start.1
  0.6 0.6 %copy-done.1 = s32[65]{0:T(128)S(1)} copy-done((s32[65]{0:T(128)S(1)}, s32[65]{0:T(128)}, u32[]{:S(2)}) %copy-start.1) | copy-done | bytes 284
  1.3 0.0 copy-start
  1.3 0.8 %copy-done = f32[8192]{0:T(1024)S(1)} copy-done((f32[8192]{0:T(1024)S(1)}, f32[8192]{0:T(1024)}, u32[]{:S(2)}) %copy-start) | copy-done | bytes 32792
  2.0 36.8 %shard_map.59 = (f32[16,2,64,128]{3,2,1,0:T(8,128)S(1)}, f32[64,128]{1,0:T(8,128)S(1)}) custom-call(f32[16,2,64,128]{3,2,1,0:T(8,128)} %bitcast.8, f32[64,128]{1,0:T(8,128)S(1)} %bitcast.6, f32[16,2,64,128]{3,2,1,0:T(8,128)} %bitcast.9, s32[1,65]{1,0:T(1,128)S(1)} %bitcast.7), custom_call_target="tpu_custom_call" | custom-call | tf_op jit(solution)/shard_map/pallas_call | solution.py:421
  38.8 1.0 %shard_map.60 = (f32[16,2,64,128]{3,2,1,0:T(8,128)}, f32[64,128]{1,0:T(8,128)}) custom-call(f32[16,2,64,128]{3,2,1,0:T(8,128)S(1)} %get-tuple-element.6.newp, f32[64,128]{1,0:T(8,128)S(1)} %get-tuple-element.7.newm), custom_call_target="tpu_custom_call" | custom-call | tf_op jit(solution)/shard_map/pallas_call | solution.py:459
Async XLA Ops:
  0.6 0.7 %copy-start.1 = (s32[65]{0:T(128)S(1)}, s32[65]{0:T(128)}, u32[]{:S(2)}) copy-start(s32[65]{0:T(128)} %param.5) | copy-start | bytes 784
  1.3 0.8 %copy-start = (f32[8192]{0:T(1024)S(1)}, f32[8192]{0:T(1024)}, u32[]{:S(2)}) copy-start(f32[8192]{0:T(1024)} %param.7) | copy-start | bytes 98308

commit v7 on v6

--- a/solution.py
+++ b/solution.py
@@ -39,6 +39,12 @@
         order.remove(half - 1)
         order.insert(half, half - 1)
     return order + [0]
+
+
+def in_pairs(terms):
+    while len(terms) > 1:
+        terms = [a + b for a, b in zip(terms[::2], terms[1::2])]
+    return terms[0]
 
 
 def step_kernel(
@@ -194,6 +200,7 @@
         low, high = ov[:, 0:tensors], ov[:, 1 : tensors + 1]
         low, high = jnp.concatenate([low, low], axis=1), jnp.concatenate([high, high], axis=1)
         lanes = 2 * tensors
+        limit = CLIP_RMS * jnp.sqrt((high - low).astype(jnp.float32))
 
         def row_mask(first_pos):
             pos = first_pos + 128 * lax.broadcasted_iota(jnp.int32, (rows, lanes), 0)
@@ -304,10 +311,7 @@
         def _():
             with scope("q1"):
                 came(all_of(sq1, ny * nc - 1), q_recv.at[0])
-                acc = sq1[0]
-                for i in range(1, ny * nc):
-                    acc = acc + sq1[i]
-                sq2[slot2] = acc
+                sq2[slot2] = in_pairs([sq1[i] for i in range(ny * nc)])
                 for dev in peers2:
                     send(sq2.at[slot2], sq2.at[slot2], q_send.at[1], q_recv.at[1], dev)
 
@@ -357,12 +361,9 @@
 
     with scope("q2"):
         came(all_of(sq2, nh * nq - 1), q_recv.at[1])
-        acc = sq2[0]
-        for i in range(1, nh * nq):
-            acc = acc + sq2[i]
+        acc = in_pairs([sq2[i] for i in range(nh * nq)])
     with scope("factor"):
-        lengths = (high - low).astype(jnp.float32)
-        factor = jnp.minimum(1.0, CLIP_RMS * jnp.sqrt(lengths) * lax.rsqrt(acc + EPSILON))
+        factor = jnp.minimum(1.0, limit * lax.rsqrt(acc + EPSILON))
         at = lambda axis: lax.broadcasted_iota(jnp.int32, (tensors, lanes), axis)
         spread = jnp.sum(jnp.where(at(0) == at(1), factor, 0.0), axis=1, keepdims=True)
         spread = jnp.broadcast_to(spread, (tensors, 128))

time: 40 us -> 40 us (level)
  no operation moved by 1% of the time
where the time goes in v7:
time: 40 us; the launch traced here: 39.7 us
  Pallas kernels  37.7 us (94%)
  local copies, waits for them, and re-layouts  1.41 us (4%)
  between operations  0.65 us (2%)
    pallas_call x1, Pallas kernels, on_device(): pl.pallas_call(functools.partial(step_kernel, sizes), out_shape=outs, in_...  36.7 us
    unnamed x4, local copies, waits for them, and re-layouts  1.41 us
    pallas_call x1, Pallas kernels, on_device(): pl.pallas_call(write_out, out_shape=outs, in_specs=list(in_vmem), out_spe...  0.99 us

profile of v7, /device:TPU:1, one launch (start us, length us, event | category | flops | bytes accessed | tf_op | source)
XLA Modules:
  0.0 39.7 jit_solution(331548860125310359)
XLA Ops:
  0.6 0.0 copy-start.1
  0.6 0.6 %copy-done.1 = s32[65]{0:T(128)S(1)} copy-done((s32[65]{0:T(128)S(1)}, s32[65]{0:T(128)}, u32[]{:S(2)}) %copy-start.1) | copy-done | bytes 284
  1.3 0.0 copy-start
  1.3 0.8 %copy-done = f32[8192]{0:T(1024)S(1)} copy-done((f32[8192]{0:T(1024)S(1)}, f32[8192]{0:T(1024)}, u32[]{:S(2)}) %copy-start) | copy-done | bytes 32792
  2.0 36.7 %shard_map.59 = (f32[16,2,64,128]{3,2,1,0:T(8,128)S(1)}, f32[64,128]{1,0:T(8,128)S(1)}) custom-call(f32[16,2,64,128]{3,2,1,0:T(8,128)} %bitcast.8, f32[64,128]{1,0:T(8,128)S(1)} %bitcast.6, f32[16,2,64,128]{3,2,1,0:T(8,128)} %bitcast.9, s32[1,65]{1,0:T(1,128)S(1)} %bitcast.7), custom_call_target="tpu_custom_call" | custom-call | tf_op jit(solution)/shard_map/pallas_call | solution.py:422
  38.8 1.0 %shard_map.60 = (f32[16,2,64,128]{3,2,1,0:T(8,128)}, f32[64,128]{1,0:T(8,128)}) custom-call(f32[16,2,64,128]{3,2,1,0:T(8,128)S(1)} %get-tuple-element.6.newp, f32[64,128]{1,0:T(8,128)S(1)} %get-tuple-element.7.newm), custom_call_target="tpu_custom_call" | custom-call | tf_op jit(solution)/shard_map/pallas_call | solution.py:460
Async XLA Ops:
  0.6 0.7 %copy-start.1 = (s32[65]{0:T(128)S(1)}, s32[65]{0:T(128)}, u32[]{:S(2)}) copy-start(s32[65]{0:T(128)} %param.5) | copy-start | bytes 784
  1.3 0.8 %copy-start = (f32[8192]{0:T(1024)S(1)}, f32[8192]{0:T(1024)}, u32[]{:S(2)}) copy-start(f32[8192]{0:T(1024)} %param.7) | copy-start | bytes 98308
